TPU v7x, 32 devices: a whole 2x2x4 slice. The times are simulated.
32 devices in a mesh: dp: 4 (over y, x), centers: 8 (over z, core).
Axes of the slice: x: 2, y: 2, z: 4, core: 2. Of those that a mesh axis runs over, the one named last changes fastest.
Arguments:
- points: bfloat16 [16384, 32], P('dp'), may hold values from -6 to 6
- centers: bfloat16 [16384, 32], P('centers'), may hold values from -6 to 6
- coef: bfloat16 [16384, 64], P('centers'), may hold values from -0.1875 to 0.1875
Outputs:
- product: float32 [16384, 64], P('centers')
All inputs are finite; a program needn't handle non-finite values.
Results may differ from a plain program's by a relative error of at most 0.0003.
Values may be sent and summed in bfloat16 or wider, within the bound.
No kernel may reach another device: no remote copies, remote signals or barrier semaphores. Data moves between devices by JAX's collectives and lax.ppermute only.
A program may use at most 128 MiB of HBM per device.

v0:
```python
import jax
import jax.numpy as jnp
from jax import lax
from jax.sharding import PartitionSpec as P


def kernel_block(left_pts, left_sq, right_pts, right_sq, features):
    inner = lax.dot_general(
        left_pts, right_pts, (((1,), (1,)), ((), ())), preferred_element_type=jnp.float32
    )
    dist = left_sq[:, None] + right_sq[None, :] - 2.0 * inner
    return jnp.exp(dist * (-2.0 / features)).astype(jnp.bfloat16)


def squares(values):
    wide = values.astype(jnp.float32)
    return jnp.sum(wide * wide, axis=1)


def on_device(points, centers, coef):
    features = points.shape[1]
    local_pts = points.shape[0]
    local_cen = centers.shape[0]
    outs_count = coef.shape[1]
    block_pts = min(1024, local_pts)
    block_count = local_pts // block_pts
    cen_sq = squares(centers)
    point_blocks = points.reshape(block_count, block_pts, features)
    scalar_zero = jnp.zeros((), jnp.float32)

    def forward_keep(carry, block):
        kernel = kernel_block(block, squares(block), centers, cen_sq, features)
        return (carry, (kernel, jnp.dot(kernel, coef, preferred_element_type=jnp.float32)))

    unused, (tiles, partial_value) = lax.scan(forward_keep, scalar_zero, point_blocks)
    forward_part = partial_value.reshape(local_pts, outs_count)
    shared = lax.psum_scatter(
        forward_part.astype(jnp.bfloat16), "centers", scatter_dimension=0, tiled=True
    )
    forward = lax.all_gather(shared, "centers", axis=0, tiled=True)
    forward_blocks = forward.reshape(block_count, block_pts, outs_count)
    back = jnp.einsum("bij,bio->jo", tiles, forward_blocks, preferred_element_type=jnp.float32)
    total_pts = local_pts * lax.axis_size("dp")
    back = back * (1.0 / jnp.sqrt(jnp.float32(total_pts)))
    own_count = local_cen // lax.axis_size("dp")
    own_start = lax.axis_index("dp") * own_count
    own_cen = lax.dynamic_slice_in_dim(centers, own_start, own_count, 0)
    own_sq = squares(own_cen)
    piece_cen = lax.all_gather(centers, "centers", axis=0, tiled=True)
    piece_coef = lax.all_gather(coef, "centers", axis=0, tiled=True)
    kernel = kernel_block(own_cen, own_sq, piece_cen, squares(piece_cen), features)
    regular = jnp.dot(kernel, piece_coef, preferred_element_type=jnp.float32)
    placed = lax.dynamic_update_slice_in_dim(jnp.zeros_like(back), regular, own_start, 0)
    return lax.psum(back + placed, "dp")


def solution(mesh):
    in_specs = (P("dp", None), P("centers", None), P("centers", None))
    out_specs = P("centers", None)
    return jax.shard_map(
        on_device, mesh=mesh, in_specs=in_specs, out_specs=out_specs, check_vma=False
    )
```

profile of v0, /device:TPU:0, one launch (start us, length us, event | category | flops | bytes accessed | tf_op | source)
XLA Modules:
  0.0 192.9 jit_solution(11572367523075643524)
XLA Ops:
  6.5 0.0 reduce-scatter.2.cloned.1.call-start
  6.5 1.4 copy.5
  8.0 1.0 multiply_reduce_fusion.2
  8.9 27.9 %while.12 = (s32[]{:T(128)}, bf16[4,1024,2048]{2,1,0:T(8,128)(2,1)}, bf16[4,1024,64]{1,2,0:T(8,128)(2,1)S(1)}, bf16[4,1024,32]{2,1,0:T(8,128)(2,1)S(1)}, f32[204...) while((s32[]{:T(128)}, bf16[4,1024,2048]{2,1,0:T(8,128)(2,1)}, ...), condition=%wide.region_3.4_spmd, body=%wide.region_1.3_spmd.sunk | while | flops 413236224 | bytes 13583461 | solution.py:35
  8.9 0.2 multiply_reduce_fusion.5
  9.2 4.4 %bitcast_dynamic-update-slice_fusion.2 = (bf16[4,1024,2048]{2,1,0:T(8,128)(2,1)}, bf16[1024,2048]{1,0:T(8,128)(2,1)S(1)}) fusion(bf16[4,1024,2048]{2,1,0:T(8,128)(2,1)} %get-tuple-element.117, s32[]{:T(128)S(6)} %copy.19, bf16[2048,32]{0,1:T(8,128)(2,1)} %get-tuple-element.129, bf16[4,1024,32]{2,1,0:T(8,128)(2,1)S(1)} %get-tuple-element.127, ...), kind=kOutput, calls=%fused_computation.1.clone.1 | convolution fusion | flops 144703488 | bytes 8795136 | tf_op jit(solution)/shard_map/while/body/eval_jaxpr/dot_general | solution.py:8
  13.5 2.3 %fusion.29 = bf16[4,1024,64]{1,2,0:T(8,128)(2,1)S(1)} fusion(bf16[4,1024,64]{1,2,0:T(8,128)(2,1)S(1)} %get-tuple-element.118, s32[]{:T(128)S(6)} %copy.19, bf16[1024,2048]{1,0:T(8,128)(2,1)S(1)} %get-tuple-element.107, bf16[2048,64]{0,1:T(8,128)(2,1)} %get-tuple-element.130), kind=kOutput, calls=%fused_computation.3.clone.1 | convolution fusion | flops 268435456 | bytes 4718596 | tf_op jit(solution)/shard_map/while/body/eval_jaxpr/dot_general | solution.py:33
  15.9 0.2 multiply_reduce_fusion.5
  16.1 4.4 %bitcast_dynamic-update-slice_fusion.2 = (bf16[4,1024,2048]{2,1,0:T(8,128)(2,1)}, bf16[1024,2048]{1,0:T(8,128)(2,1)S(1)}) fusion(bf16[4,1024,2048]{2,1,0:T(8,128)(2,1)} %get-tuple-element.117, s32[]{:T(128)S(6)} %copy.19, bf16[2048,32]{0,1:T(8,128)(2,1)} %get-tuple-element.129, bf16[4,1024,32]{2,1,0:T(8,128)(2,1)S(1)} %get-tuple-element.127, ...), kind=kOutput, calls=%fused_computation.1.clone.1 | convolution fusion | flops 144703488 | bytes 8795136 | tf_op jit(solution)/shard_map/while/body/eval_jaxpr/dot_general | solution.py:8
  20.5 2.3 %fusion.29 = bf16[4,1024,64]{1,2,0:T(8,128)(2,1)S(1)} fusion(bf16[4,1024,64]{1,2,0:T(8,128)(2,1)S(1)} %get-tuple-element.118, s32[]{:T(128)S(6)} %copy.19, bf16[1024,2048]{1,0:T(8,128)(2,1)S(1)} %get-tuple-element.107, bf16[2048,64]{0,1:T(8,128)(2,1)} %get-tuple-element.130), kind=kOutput, calls=%fused_computation.3.clone.1 | convolution fusion | flops 268435456 | bytes 4718596 | tf_op jit(solution)/shard_map/while/body/eval_jaxpr/dot_general | solution.py:33
  22.9 0.2 multiply_reduce_fusion.5
  23.1 4.4 %bitcast_dynamic-update-slice_fusion.2 = (bf16[4,1024,2048]{2,1,0:T(8,128)(2,1)}, bf16[1024,2048]{1,0:T(8,128)(2,1)S(1)}) fusion(bf16[4,1024,2048]{2,1,0:T(8,128)(2,1)} %get-tuple-element.117, s32[]{:T(128)S(6)} %copy.19, bf16[2048,32]{0,1:T(8,128)(2,1)} %get-tuple-element.129, bf16[4,1024,32]{2,1,0:T(8,128)(2,1)S(1)} %get-tuple-element.127, ...), kind=kOutput, calls=%fused_computation.1.clone.1 | convolution fusion | flops 144703488 | bytes 8795136 | tf_op jit(solution)/shard_map/while/body/eval_jaxpr/dot_general | solution.py:8
  27.5 2.3 %fusion.29 = bf16[4,1024,64]{1,2,0:T(8,128)(2,1)S(1)} fusion(bf16[4,1024,64]{1,2,0:T(8,128)(2,1)S(1)} %get-tuple-element.118, s32[]{:T(128)S(6)} %copy.19, bf16[1024,2048]{1,0:T(8,128)(2,1)S(1)} %get-tuple-element.107, bf16[2048,64]{0,1:T(8,128)(2,1)} %get-tuple-element.130), kind=kOutput, calls=%fused_computation.3.clone.1 | convolution fusion | flops 268435456 | bytes 4718596 | tf_op jit(solution)/shard_map/while/body/eval_jaxpr/dot_general | solution.py:33
  29.8 0.2 multiply_reduce_fusion.5
  30.1 4.4 %bitcast_dynamic-update-slice_fusion.2 = (bf16[4,1024,2048]{2,1,0:T(8,128)(2,1)}, bf16[1024,2048]{1,0:T(8,128)(2,1)S(1)}) fusion(bf16[4,1024,2048]{2,1,0:T(8,128)(2,1)} %get-tuple-element.117, s32[]{:T(128)S(6)} %copy.19, bf16[2048,32]{0,1:T(8,128)(2,1)} %get-tuple-element.129, bf16[4,1024,32]{2,1,0:T(8,128)(2,1)S(1)} %get-tuple-element.127, ...), kind=kOutput, calls=%fused_computation.1.clone.1 | convolution fusion | flops 144703488 | bytes 8795136 | tf_op jit(solution)/shard_map/while/body/eval_jaxpr/dot_general | solution.py:8
  34.5 2.3 %fusion.29 = bf16[4,1024,64]{1,2,0:T(8,128)(2,1)S(1)} fusion(bf16[4,1024,64]{1,2,0:T(8,128)(2,1)S(1)} %get-tuple-element.118, s32[]{:T(128)S(6)} %copy.19, bf16[1024,2048]{1,0:T(8,128)(2,1)S(1)} %get-tuple-element.107, bf16[2048,64]{0,1:T(8,128)(2,1)} %get-tuple-element.130), kind=kOutput, calls=%fused_computation.3.clone.1 | convolution fusion | flops 268435456 | bytes 4718596 | tf_op jit(solution)/shard_map/while/body/eval_jaxpr/dot_general | solution.py:33
  36.8 0.8 copy.9
  37.7 0.0 reduce-scatter.2.cloned.1.call-update
  37.7 0.0 all-gather.3.cloned.1.call-start
  37.7 0.7 all-gather.3.cloned.1.call-update
  38.4 0.0 all-gather.5.cloned.1.call-start
  38.5 0.7 all-gather.5.cloned.1.call-update
  39.2 0.0 all-reduce.2.cloned.1.call-start
  39.2 0.8 multiply_reduce_fusion.3
  40.0 31.9 %reduce-scatter.2.cloned.1.call-done = bf16[512,64]{0,1:T(8,128)(2,1)} async-done(((bf16[4096,64]{0,1:T(8,128)(2,1)}), bf16[512,64]{0,1:T(8,128)(2,1)}) %reduce-scatter.2.cloned.1.call-update) | async-done | bytes 65552 | tf_op jit(solution)/shard_map/reduce_scatter | solution.py:37
  71.9 16.8 %all_gather.9 = bf16[4096,64]{0,1:T(8,128)(2,1)S(1)} all-gather(bf16[512,64]{0,1:T(8,128)(2,1)} %reduce-scatter.2.cloned.1.call-done), channel_id=1, replica_groups=mesh['dp'=4,'centers'=8] {'centers'}, dimensions={0}, use_global_device_ids=true | all-gather | bytes 589824 | tf_op jit(solution)/shard_map/all_gather | solution.py:40
  88.7 8.9 %fusion.5 = f32[2048,64]{0,1:T(8,128)S(1)} fusion(bf16[4,1024,2048]{2,1,0:T(8,128)(2,1)} %get-tuple-element.43, bf16[8,4,8,1024]{3,2,1,0:T(8,128)(2,1)S(1)} %bitcast.46), kind=kOutput, calls=%fused_computation.11 | convolution fusion | flops 1073872896 | bytes 17825792 | tf_op jit(solution)/shard_map/bij,bio->jo/dot_general | solution.py:42
  97.6 0.0 all-gather.3.cloned.1.call-done
  97.6 1.5 multiply_reduce_fusion.1
  99.2 26.4 %all-gather.5.cloned.1.call-done = bf16[16384,64]{0,1:T(8,128)(2,1)} async-done(((bf16[2048,64]{0,1:T(8,128)(2,1)}), bf16[16384,64]{0,1:T(8,128)(2,1)}) %all-gather.5.cloned.1.call-update) | async-done | bytes 2097168 | tf_op jit(solution)/shard_map/all_gather | solution.py:50
  125.6 13.2 %fusion.7 = f32[2048,64]{0,1:T(8,128)S(1)} fusion(f32[2048,64]{0,1:T(8,128)S(1)} %fusion.5, s32[]{:T(128)S(6)} %select_n.4, bf16[16384,64]{0,1:T(8,128)(2,1)} %all-gather.5.cloned.1.call-done, bf16[16384,32]{0,1:T(8,128)(2,1)} %all-gather.3.cloned.1.call-done, f32[16384]{0:T(1024)S(1)} %multiply_reduce_fusion.1, f32[512]{0:T(512)S(1)} %multiply_reduce_fusion.3, ...), kind=kOutput, calls=%fused_computation.14 | convolution fusion | flops 1652588544 | bytes 3509248 | tf_op jit(solution)/shard_map/dot_general | solution.py:52
  138.8 0.0 copy-start
  138.8 0.8 copy-done
  139.6 0.0 all-reduce.2.cloned.1.call-update
  139.6 44.9 %all-reduce.2.cloned.1.call-done = f32[2048,64]{0,1:T(8,128)} async-done(((f32[2048,64]{0,1:T(8,128)}), f32[2048,64]{0,1:T(8,128)}) %all-reduce.2.cloned.1.call-update) | async-done | bytes 524304 | tf_op jit(solution)/shard_map/psum | solution.py:54
  184.5 1.9 copy.27
  (2 shorter events, 0.0 us)
Async XLA Ops:
  6.5 65.4 %reduce-scatter.2.cloned.1.call-start = ((), (), s32[]{:S(2)}) async-start(), calls=%async_computation.1 | async-start | bytes 589824 | tf_op jit(solution)/shard_map/reduce_scatter | solution.py:37
  37.7 59.9 %all-gather.3.cloned.1.call-start = ((), (), s32[]{:S(2)}) async-start(), calls=%async_computation.2 | async-start | bytes 1179648 | tf_op jit(solution)/shard_map/all_gather | solution.py:49
  38.4 87.2 %all-gather.5.cloned.1.call-start = ((), (), s32[]{:S(2)}) async-start(), calls=%async_computation.3 | async-start | bytes 2359296 | tf_op jit(solution)/shard_map/all_gather | solution.py:50
  39.2 145.4 %all-reduce.2.cloned.1.call-start = ((), (), s32[]{:S(2)}) async-start(), calls=%async_computation.4 | async-start | bytes 1048576 | tf_op jit(solution)/shard_map/psum | solution.py:54
  138.8 0.8 copy-start
Sparse Core Ops, SparseCore 0:
  37.8 34.0 reduce-scatter.1
  73.5 21.7 all-gather.2
  96.9 28.6 all-gather.4
  139.7 44.7 all-reduce.1
where the time goes:
time: 193 us
  waiting for transfers between devices  105 us (54%)
  matrix products  49 us (25%)
  blocking collectives  16.8 us (9%)
  between operations  13.2 us (7%)
  local copies, waits for them, and re-layouts  4.92 us (3%)
  other arithmetic  4.13 us (2%)
    psum x1, waiting for transfers between devices, on_device(): return lax.psum(back + placed, 'dp')  44.9 us
    reduce_scatter x1, waiting for transfers between devices, on_device(): lax.psum_scatter(forward_part.astype(jnp.bfloat16), 'centers', scatter_di...  31.9 us
    all_gather x1, waiting for transfers between devices, on_device(): piece_coef = lax.all_gather(coef, 'centers', axis=0, tiled=True)  26.4 us
    dot_general x4, matrix products, kernel_block(): lax.dot_general(left_pts, right_pts, (((1,), (1,)), ((), ())), preferred_...  17.6 us
    all_gather x1, blocking collectives, on_device(): forward = lax.all_gather(shared, 'centers', axis=0, tiled=True)  16.8 us
    dot_general x1, matrix products, on_device(): regular = jnp.dot(kernel, piece_coef, preferred_element_type=jnp.float32)  13.2 us
    dot_general x4, matrix products, forward_keep(): jnp.dot(kernel, coef, preferred_element_type=jnp.float32)  9.35 us
    dot_general x1, matrix products, on_device(): jnp.einsum('bij,bio->jo', tiles, forward_blocks, preferred_element_type=j...  8.89 us
  transfers between devices with their start and end apart: 4, of which 3 were waited for; matrix products, arithmetic and copies ran while one was open for 6% of the time, Pallas kernels for 0%

commit v1 on v0

--- a/solution.py
+++ b/solution.py
@@ -47,7 +47,13 @@
     own_cen = lax.dynamic_slice_in_dim(centers, own_start, own_count, 0)
     own_sq = squares(own_cen)
     piece_cen = lax.all_gather(centers, "centers", axis=0, tiled=True)
-    piece_coef = lax.all_gather(coef, "centers", axis=0, tiled=True)
+    size = lax.axis_size("centers")
+    block_2, shards = (coef, [coef])
+    for _ in range(size - 1):
+        block_2 = lax.ppermute(block_2, "centers", [(i, (i + 1) % size) for i in range(size)])
+        shards.insert(0, block_2)
+    merged = jnp.concatenate(shards, axis=0)
+    piece_coef = jnp.roll(merged, (lax.axis_index("centers") + 1) * coef.shape[0], axis=0)
     kernel = kernel_block(own_cen, own_sq, piece_cen, squares(piece_cen), features)
     regular = jnp.dot(kernel, piece_coef, preferred_element_type=jnp.float32)
     placed = lax.dynamic_update_slice_in_dim(jnp.zeros_like(back), regular, own_start, 0)

time: 193 us -> 181 us (0.938)
  waiting for transfers between devices: 105 us -> 84.3 us
  local copies, waits for them, and re-layouts: 4.92 us -> 16.5 us
  matrix products: 49 us -> 45.4 us
    ppermute x0 -> x7, waiting for transfers between devices: none -> 29.5 us  [on_device(): lax.ppermute(block_2, 'centers', [(i, (i + 1) % size) for i in range(size)])]
    all_gather x1 -> x0, waiting for transfers between devices: 26.4 us -> none  [on_device(): piece_coef = lax.all_gather(coef, 'centers', axis=0, tiled=True)]
    reduce_scatter x1, waiting for transfers between devices: 31.9 us -> 8.35 us  [on_device(): lax.psum_scatter(forward_part.astype(jnp.bfloat16), 'centers', scatter_di...]
    unnamed x4 -> x21, local copies, waits for them, and re-layouts: 4.08 us -> 14.9 us
    dot_general x4, matrix products: 9.35 us -> 5.56 us  [forward_keep(): jnp.dot(kernel, coef, preferred_element_type=jnp.float32)]
  transfers between devices with their start and end apart: 4 -> 10, of which waited for: 3 -> 6; matrix products, arithmetic and copies ran while one was open for 6% -> 27% of each run, Pallas kernels for 0% -> 0%
where the time goes in v1:
time: 181 us
  waiting for transfers between devices  84.3 us (47%)
  matrix products  45.4 us (25%)
  local copies, waits for them, and re-layouts  16.5 us (9%)
  blocking collectives  15.9 us (9%)
  between operations  13.2 us (7%)
  other arithmetic  4.13 us (2%)
    psum x1, waiting for transfers between devices, on_device(): return lax.psum(back + placed, 'dp')  46.4 us
    ppermute x7, waiting for transfers between devices, on_device(): lax.ppermute(block_2, 'centers', [(i, (i + 1) % size) for i in range(size)])  29.5 us
    dot_general x4, matrix products, kernel_block(): lax.dot_general(left_pts, right_pts, (((1,), (1,)), ((), ())), preferred_...  17.8 us
    all_gather x1, blocking collectives, on_device(): forward = lax.all_gather(shared, 'centers', axis=0, tiled=True)  15.9 us
    unnamed x21, local copies, waits for them, and re-layouts  14.9 us
    dot_general x1, matrix products, on_device(): regular = jnp.dot(kernel, piece_coef, preferred_element_type=jnp.float32)  13.2 us
    dot_general x1, matrix products, on_device(): jnp.einsum('bij,bio->jo', tiles, forward_blocks, preferred_element_type=j...  8.95 us
    reduce_scatter x1, waiting for transfers between devices, on_device(): lax.psum_scatter(forward_part.astype(jnp.bfloat16), 'centers', scatter_di...  8.35 us
  transfers between devices with their start and end apart: 10, of which 6 were waited for; matrix products, arithmetic and copies ran while one was open for 27% of the time, Pallas kernels for 0%

profile of v1, /device:TPU:0, one launch (start us, length us, event | category | flops | bytes accessed | tf_op | source)
XLA Modules:
  0.0 180.9 jit_solution(2198921239967663574)
XLA Ops:
  6.5 0.5 collective-permute-start
  7.0 1.4 copy.5
  8.5 1.0 multiply_reduce_fusion.2
  9.4 5.9 %collective-permute-done = bf16[2048,64]{0,1:T(8,128)(2,1)S(1)} collective-permute-done((bf16[2048,64]{0,1:T(8,128)(2,1)}, bf16[2048,64]{0,1:T(8,128)(2,1)S(1)}, u32[]{:S(2)}, u32[]{:S(2)}) %collective-permute-start) | collective-permute-done | bytes 262176 | tf_op jit(solution)/shard_map/ppermute | solution.py:53
  15.3 0.0 collective-permute-start.1
  15.3 24.3 %while.12 = (s32[]{:T(128)}, bf16[4,1024,2048]{2,1,0:T(8,128)(2,1)}, bf16[4,1024,64]{1,2,0:T(8,128)(2,1)S(1)}, bf16[4,1024,32]{2,1,0:T(8,128)(2,1)S(1)}, f32[204...) while((s32[]{:T(128)}, bf16[4,1024,2048]{2,1,0:T(8,128)(2,1)}, ...), condition=%wide.region_3.4_spmd, body=%wide.region_1.3_spmd.sunk | while | flops 413236224 | bytes 14632065 | solution.py:35
  15.3 0.2 multiply_reduce_fusion.5
  15.5 0.0 copy-start
  15.6 4.4 %bitcast_dynamic-update-slice_fusion.2 = (bf16[4,1024,2048]{2,1,0:T(8,128)(2,1)}, bf16[1024,2048]{1,0:T(8,128)(2,1)S(1)}) fusion(bf16[4,1024,2048]{2,1,0:T(8,128)(2,1)} %get-tuple-element.117, s32[]{:T(128)S(6)} %copy.19, bf16[2048,32]{0,1:T(8,128)(2,1)} %get-tuple-element.129, bf16[4,1024,32]{2,1,0:T(8,128)(2,1)S(1)} %get-tuple-element.127, ...), kind=kOutput, calls=%fused_computation.1.clone.1 | convolution fusion | flops 144703488 | bytes 8795136 | tf_op jit(solution)/shard_map/while/body/eval_jaxpr/dot_general | solution.py:8
  20.0 1.4 fusion.33
  21.4 0.2 multiply_reduce_fusion.5
  21.6 0.0 copy-start
  21.6 4.5 %bitcast_dynamic-update-slice_fusion.2 = (bf16[4,1024,2048]{2,1,0:T(8,128)(2,1)}, bf16[1024,2048]{1,0:T(8,128)(2,1)S(1)}) fusion(bf16[4,1024,2048]{2,1,0:T(8,128)(2,1)} %get-tuple-element.117, s32[]{:T(128)S(6)} %copy.19, bf16[2048,32]{0,1:T(8,128)(2,1)} %get-tuple-element.129, bf16[4,1024,32]{2,1,0:T(8,128)(2,1)S(1)} %get-tuple-element.127, ...), kind=kOutput, calls=%fused_computation.1.clone.1 | convolution fusion | flops 144703488 | bytes 8795136 | tf_op jit(solution)/shard_map/while/body/eval_jaxpr/dot_general | solution.py:8
  26.1 1.4 fusion.33
  27.5 0.2 multiply_reduce_fusion.5
  27.7 0.0 copy-start
  27.7 4.4 %bitcast_dynamic-update-slice_fusion.2 = (bf16[4,1024,2048]{2,1,0:T(8,128)(2,1)}, bf16[1024,2048]{1,0:T(8,128)(2,1)S(1)}) fusion(bf16[4,1024,2048]{2,1,0:T(8,128)(2,1)} %get-tuple-element.117, s32[]{:T(128)S(6)} %copy.19, bf16[2048,32]{0,1:T(8,128)(2,1)} %get-tuple-element.129, bf16[4,1024,32]{2,1,0:T(8,128)(2,1)S(1)} %get-tuple-element.127, ...), kind=kOutput, calls=%fused_computation.1.clone.1 | convolution fusion | flops 144703488 | bytes 8795136 | tf_op jit(solution)/shard_map/while/body/eval_jaxpr/dot_general | solution.py:8
  32.2 1.4 fusion.33
  33.6 0.2 multiply_reduce_fusion.5
  33.8 0.0 copy-start
  33.8 4.4 %bitcast_dynamic-update-slice_fusion.2 = (bf16[4,1024,2048]{2,1,0:T(8,128)(2,1)}, bf16[1024,2048]{1,0:T(8,128)(2,1)S(1)}) fusion(bf16[4,1024,2048]{2,1,0:T(8,128)(2,1)} %get-tuple-element.117, s32[]{:T(128)S(6)} %copy.19, bf16[2048,32]{0,1:T(8,128)(2,1)} %get-tuple-element.129, bf16[4,1024,32]{2,1,0:T(8,128)(2,1)S(1)} %get-tuple-element.127, ...), kind=kOutput, calls=%fused_computation.1.clone.1 | convolution fusion | flops 144703488 | bytes 8795136 | tf_op jit(solution)/shard_map/while/body/eval_jaxpr/dot_general | solution.py:8
  38.2 1.4 fusion.33
  39.6 0.8 copy.9
  40.5 0.0 reduce-scatter.2.cloned.1.call-update
  40.5 0.0 all-gather.2.cloned.1.call-start
  40.5 0.0 collective-permute-done.1
  40.5 0.4 collective-permute-start.2
  41.0 7.2 %collective-permute-done.2 = bf16[2048,64]{0,1:T(8,128)(2,1)S(1)} collective-permute-done((bf16[2048,64]{0,1:T(8,128)(2,1)S(1)}, bf16[2048,64]{0,1:T(8,128)(2,1)S(1)}, u32[]{:S(2)}, u32[]{:S(2)}) %collective-permute-start.2) | collective-permute-done | bytes 262176 | tf_op jit(solution)/shard_map/ppermute | solution.py:53
  48.2 0.0 collective-permute-start.3
  48.2 8.3 %collective-permute-done.3 = bf16[2048,64]{0,1:T(8,128)(2,1)S(1)} collective-permute-done((bf16[2048,64]{0,1:T(8,128)(2,1)S(1)}, bf16[2048,64]{0,1:T(8,128)(2,1)S(1)}, u32[]{:S(2)}, u32[]{:S(2)}) %collective-permute-start.3) | collective-permute-done | bytes 262176 | tf_op jit(solution)/shard_map/ppermute | solution.py:53
  56.5 0.0 collective-permute-start.4
  56.5 8.1 %collective-permute-done.4 = bf16[2048,64]{0,1:T(8,128)(2,1)S(1)} collective-permute-done((bf16[2048,64]{0,1:T(8,128)(2,1)S(1)}, bf16[2048,64]{0,1:T(8,128)(2,1)S(1)}, u32[]{:S(2)}, u32[]{:S(2)}) %collective-permute-start.4) | collective-permute-done | bytes 262176 | tf_op jit(solution)/shard_map/ppermute | solution.py:53
  64.6 0.0 collective-permute-start.5
  64.6 0.0 all-gather.2.cloned.1.call-update
  64.6 0.0 all-reduce.2.cloned.1.call-start
  64.7 0.8 multiply_reduce_fusion.3
  65.5 8.4 %reduce-scatter.2.cloned.1.call-done = bf16[512,64]{0,1:T(8,128)(2,1)} async-done(((bf16[4096,64]{0,1:T(8,128)(2,1)}), bf16[512,64]{0,1:T(8,128)(2,1)}) %reduce-scatter.2.cloned.1.call-update) | async-done | bytes 65552 | tf_op jit(solution)/shard_map/reduce_scatter | solution.py:37
  73.8 15.9 %all_gather.6 = bf16[4096,64]{0,1:T(8,128)(2,1)S(1)} all-gather(bf16[512,64]{0,1:T(8,128)(2,1)} %reduce-scatter.2.cloned.1.call-done), channel_id=1, replica_groups=mesh['dp'=4,'centers'=8] {'centers'}, dimensions={0}, use_global_device_ids=true | all-gather | bytes 589824 | tf_op jit(solution)/shard_map/all_gather | solution.py:40
  89.7 0.0 collective-permute-done.5
  89.8 0.3 collective-permute-start.6
  90.1 8.9 %fusion.5 = f32[2048,64]{0,1:T(8,128)S(1)} fusion(bf16[4,1024,2048]{2,1,0:T(8,128)(2,1)} %get-tuple-element.43, bf16[8,4,8,1024]{3,2,1,0:T(8,128)(2,1)S(1)} %bitcast.45), kind=kOutput, calls=%fused_computation.11 | convolution fusion | flops 1073872896 | bytes 17825792 | tf_op jit(solution)/shard_map/bij,bio->jo/dot_general | solution.py:42
  99.1 0.7 constant_dynamic-update-slice_fusion.15
  99.8 0.7 constant_dynamic-update-slice_fusion.14
  100.5 0.7 constant_dynamic-update-slice_fusion.13
  101.2 0.7 constant_dynamic-update-slice_fusion.12
  101.9 0.7 constant_dynamic-update-slice_fusion.11
  102.6 0.7 constant_dynamic-update-slice_fusion.10
  103.3 0.7 constant_dynamic-update-slice_fusion.9
  104.1 0.7 constant_dynamic-update-slice_fusion.8
  104.8 0.7 constant_dynamic-update-slice_fusion.7
  105.5 0.7 constant_dynamic-update-slice_fusion.6
  106.2 0.7 constant_dynamic-update-slice_fusion.5
  106.9 0.7 constant_dynamic-update-slice_fusion.4
  107.7 0.8 constant_dynamic-update-slice_fusion.3
  108.4 0.7 constant_dynamic-update-slice_fusion.2
  109.1 0.7 constant_dynamic-update-slice_fusion.1
  109.8 0.7 constant_dynamic-update-slice_fusion
  110.6 1.5 multiply_reduce_fusion.1
  112.1 13.2 %fusion.10 = f32[2048,64]{0,1:T(8,128)S(1)} fusion(f32[2048,64]{0,1:T(8,128)S(1)} %fusion.5, s32[]{:T(128)S(6)} %select_n.17, bf16[32768,64]{0,1:T(8,128)(2,1)} %constant_dynamic-update-slice_fusion, s32[]{:T(128)S(6)} %select_n.19, bf16[16384,32]{0,1:T(8,128)(2,1)} %all-gather.2.cloned.1.call-done, f32[16384]{0:T(1024)S(1)} %multiply_reduce_fusion.1, ...), kind=kOutput, calls=%fused_computation.15 | convolution fusion | flops 1652588544 | bytes 3509760 | tf_op jit(solution)/shard_map/dot_general | solution.py:58
  125.3 0.0 copy-start.2
  125.3 0.8 copy-done.2
  126.1 0.0 all-reduce.2.cloned.1.call-update
  126.1 46.4 %all-reduce.2.cloned.1.call-done = f32[2048,64]{0,1:T(8,128)} async-done(((f32[2048,64]{0,1:T(8,128)}), f32[2048,64]{0,1:T(8,128)}) %all-reduce.2.cloned.1.call-update) | async-done | bytes 524304 | tf_op jit(solution)/shard_map/psum | solution.py:60
  172.5 1.9 %copy.42 = f32[2048,64]{0,1:T(8,128)} copy(f32[2048,64]{0,1:T(8,128)} %all-reduce.2.cloned.1.call-done) | data formatting | bytes 1048576
  (11 shorter events, 0.0 us)
Async XLA Ops:
  6.5 67.3 %reduce-scatter.2.cloned.1.call-start = ((), (), s32[]{:S(2)}) async-start(), calls=%async_computation.1 | async-start | bytes 589824 | tf_op jit(solution)/shard_map/reduce_scatter | solution.py:37
  6.5 8.8 %collective-permute-start = (bf16[2048,64]{0,1:T(8,128)(2,1)}, bf16[2048,64]{0,1:T(8,128)(2,1)S(1)}, u32[]{:S(2)}, u32[]{:S(2)}) collective-permute-start(bf16[2048,64]{0,1:T(8,128)(2,1)} %param.7), channel_id=1, source_target_pairs={{0,1},{1,2},{2,3},{3,4},{4,5},{5,6},{6,7},{7,0},{8,9},{9,10},{10,1... | collective-permute-start | bytes 786440 | tf_op jit(solution)/shard_map/ppermute | solution.py:53
  15.3 25.2 %collective-permute-start.1 = (bf16[2048,64]{0,1:T(8,128)(2,1)S(1)}, bf16[2048,64]{0,1:T(8,128)(2,1)S(1)}, u32[]{:S(2)}, u32[]{:S(2)}) collective-permute-start(bf16[2048,64]{0,1:T(8,128)(2,1)S(1)} %collective-permute-done), channel_id=1, source_target_pairs={{0,1},{1,2},{2,3},{3,4},{4,5},{5,6},{6,7},{7,0},{8,9},{9,10},{10,1... | collective-permute-start | bytes 786440 | tf_op jit(solution)/shard_map/ppermute | solution.py:53
  15.5 4.4 %copy-start = (bf16[2048,64]{0,1:T(8,128)(2,1)S(1)}, bf16[2048,64]{0,1:T(8,128)(2,1)}, u32[]{:S(2)}) copy-start(bf16[2048,64]{0,1:T(8,128)(2,1)} %get-tuple-element.130) | copy-start | bytes 786436 | tf_op jit(solution)/shard_map/while
  21.6 4.5 %copy-start = (bf16[2048,64]{0,1:T(8,128)(2,1)S(1)}, bf16[2048,64]{0,1:T(8,128)(2,1)}, u32[]{:S(2)}) copy-start(bf16[2048,64]{0,1:T(8,128)(2,1)} %get-tuple-element.130) | copy-start | bytes 786436 | tf_op jit(solution)/shard_map/while
  27.7 4.4 %copy-start = (bf16[2048,64]{0,1:T(8,128)(2,1)S(1)}, bf16[2048,64]{0,1:T(8,128)(2,1)}, u32[]{:S(2)}) copy-start(bf16[2048,64]{0,1:T(8,128)(2,1)} %get-tuple-element.130) | copy-start | bytes 786436 | tf_op jit(solution)/shard_map/while
  33.8 4.4 %copy-start = (bf16[2048,64]{0,1:T(8,128)(2,1)S(1)}, bf16[2048,64]{0,1:T(8,128)(2,1)}, u32[]{:S(2)}) copy-start(bf16[2048,64]{0,1:T(8,128)(2,1)} %get-tuple-element.130) | copy-start | bytes 786436 | tf_op jit(solution)/shard_map/while
  40.5 70.1 %all-gather.2.cloned.1.call-start = ((), (), s32[]{:S(2)}) async-start(), calls=%async_computation.2 | async-start | bytes 1179648 | tf_op jit(solution)/shard_map/all_gather | solution.py:49
  40.5 7.7 %collective-permute-start.2 = (bf16[2048,64]{0,1:T(8,128)(2,1)S(1)}, bf16[2048,64]{0,1:T(8,128)(2,1)S(1)}, u32[]{:S(2)}, u32[]{:S(2)}) collective-permute-start(bf16[2048,64]{0,1:T(8,128)(2,1)S(1)} %collective-permute-done.1), channel_id=1, source_target_pairs={{0,1},{1,2},{2,3},{3,4},{4,5},{5,6},{6,7},{7,0},{8,9},{9,10},{10,1... | collective-permute-start | bytes 786440 | tf_op jit(solution)/shard_map/ppermute | solution.py:53
  48.2 8.3 %collective-permute-start.3 = (bf16[2048,64]{0,1:T(8,128)(2,1)S(1)}, bf16[2048,64]{0,1:T(8,128)(2,1)S(1)}, u32[]{:S(2)}, u32[]{:S(2)}) collective-permute-start(bf16[2048,64]{0,1:T(8,128)(2,1)S(1)} %collective-permute-done.2), channel_id=1, source_target_pairs={{0,1},{1,2},{2,3},{3,4},{4,5},{5,6},{6,7},{7,0},{8,9},{9,10},{10,1... | collective-permute-start | bytes 786440 | tf_op jit(solution)/shard_map/ppermute | solution.py:53
  56.5 8.1 %collective-permute-start.4 = (bf16[2048,64]{0,1:T(8,128)(2,1)S(1)}, bf16[2048,64]{0,1:T(8,128)(2,1)S(1)}, u32[]{:S(2)}, u32[]{:S(2)}) collective-permute-start(bf16[2048,64]{0,1:T(8,128)(2,1)S(1)} %collective-permute-done.3), channel_id=1, source_target_pairs={{0,1},{1,2},{2,3},{3,4},{4,5},{5,6},{6,7},{7,0},{8,9},{9,10},{10,1... | collective-permute-start | bytes 786440 | tf_op jit(solution)/shard_map/ppermute | solution.py:53
  64.6 25.2 %collective-permute-start.5 = (bf16[2048,64]{0,1:T(8,128)(2,1)S(1)}, bf16[2048,64]{0,1:T(8,128)(2,1)S(1)}, u32[]{:S(2)}, u32[]{:S(2)}) collective-permute-start(bf16[2048,64]{0,1:T(8,128)(2,1)S(1)} %collective-permute-done.4), channel_id=1, source_target_pairs={{0,1},{1,2},{2,3},{3,4},{4,5},{5,6},{6,7},{7,0},{8,9},{9,10},{10,1... | collective-permute-start | bytes 786440 | tf_op jit(solution)/shard_map/ppermute | solution.py:53
  64.6 107.9 %all-reduce.2.cloned.1.call-start = ((), (), s32[]{:S(2)}) async-start(), calls=%async_computation.3 | async-start | bytes 1048576 | tf_op jit(solution)/shard_map/psum | solution.py:60
  89.8 9.3 %collective-permute-start.6 = (bf16[2048,64]{0,1:T(8,128)(2,1)S(1)}, bf16[2048,64]{0,1:T(8,128)(2,1)S(1)}, u32[]{:S(2)}, u32[]{:S(2)}) collective-permute-start(bf16[2048,64]{0,1:T(8,128)(2,1)S(1)} %collective-permute-done.5), channel_id=1, source_target_pairs={{0,1},{1,2},{2,3},{3,4},{4,5},{5,6},{6,7},{7,0},{8,9},{9,10},{10,1... | collective-permute-start | bytes 786440 | tf_op jit(solution)/shard_map/ppermute | solution.py:53
  90.1 14.0 %copy-start.1 = (bf16[2048,64]{0,1:T(8,128)(2,1)S(1)}, bf16[2048,64]{0,1:T(8,128)(2,1)}, u32[]{:S(2)}) copy-start(bf16[2048,64]{0,1:T(8,128)(2,1)} %get-tuple-element.136) | copy-start | bytes 786436
  125.3 0.8 copy-start.2
Sparse Core Ops, SparseCore 0:
  40.6 33.1 reduce-scatter.1
  75.4 22.1 all-gather.1
  126.2 46.2 all-reduce.1
